TPU v7x, 256 devices: a whole 4x4x8 slice. The times are simulated.
256 devices in a mesh: seq: 32 (over x, z), tensor: 8 (over y, core).
Axes of the slice: x: 4, y: 4, z: 8, core: 2. Of those that a mesh axis runs over, the one named last changes fastest.
Arguments:
- hidden_in: bfloat16 [12288, 4096], P('seq', 'tensor'), may hold values from -6 to 6
- norm_gain: float32 [4096], replicated, may hold values from 0.5 to 1.5
- w_x: bfloat16 [4096, 8192], P('seq', 'tensor'), may hold values from -0.09375 to 0.09375
- w_z: bfloat16 [4096, 8192], P('seq', 'tensor'), may hold values from -0.09375 to 0.09375
- w_bc: bfloat16 [4096, 8, 256], P('seq', 'tensor'), may hold values from -0.09375 to 0.09375
- w_dt: bfloat16 [4096, 64], P('seq', 'tensor'), may hold values from -0.09375 to 0.09375
- dt_bias: float32 [64], P('tensor'), may hold values from -6 to -2
- decay_rate: float32 [64], P('tensor'), may hold values from 8.138021e-05 to 8
- conv_x: float32 [4, 8192], P(None, 'tensor'), may hold values from -3 to 3
- conv_bc: float32 [4, 8, 256], P(None, 'tensor'), may hold values from -3 to 3
- conv_bias_x: float32 [8192], P('tensor'), may hold values from -3 to 3
- conv_bias_bc: float32 [8, 256], P('tensor'), may hold values from -3 to 3
- skip_d: float32 [64], P('tensor'), may hold values from 0.5 to 8
- out_gain: float32 [8192], P('tensor'), may hold values from 0.5 to 1.5
- w_out: bfloat16 [8192, 4096], P('tensor'), may hold values from -0.0625 to 0.0625
Outputs:
- layer_out: bfloat16 [12288, 4096], P('seq', 'tensor')
All inputs are finite; a program needn't handle non-finite values.
Results may differ from a plain program's by a relative error of at most 0.0095.
Values may be sent and summed in bfloat16 or wider, within the bound.
No kernel may reach another device: no remote copies, remote signals or barrier semaphores. Data moves between devices by JAX's collectives and lax.ppermute only.
A program may use at most 128 MiB of HBM per device.

v0:
```python
import math
import jax
import jax.numpy as jnp
from jax import lax
from jax.sharding import Mesh
from jax.sharding import PartitionSpec as P

SPAN = 128
SEQ = ("seq_0", "seq_1")
epsilon = 1e-05


def side_by_side(arrays, axis, dim, along):
    widths = [math.prod(a.shape[along:]) for a in arrays]
    both = jnp.concatenate(
        [a.reshape(*a.shape[:along], w) for a, w in zip(arrays, widths)], axis=along
    )
    whole = lax.all_gather(both, axis, axis=dim, tiled=True)
    tiles = jnp.split(whole, [sum(widths[:k]) for k in range(1, len(widths))], axis=along)
    return tuple((b.reshape(*whole.shape[:along], *a.shape[along:]) for a, b in zip(arrays, tiles)))


def passed_along(block, axis, distance):
    devices = range(lax.axis_size(axis))
    route = [(i - distance, i) for i in devices if i - distance in devices]
    return lax.ppermute(block, axis, route)


def nothing_yet(array, identity):
    return jax.tree.map(
        lambda a, e: jnp.broadcast_to(jnp.asarray(e, a.dtype), a.shape), array, identity
    )


def entering(array, axes, combine, identity):
    before = start = nothing_yet(array, identity)
    running = array
    for axis in reversed(axes):
        peers, place = (lax.axis_size(axis), lax.axis_index(axis))
        pieces = jax.tree.map(lambda part: lax.all_gather(part, axis), running)
        inside, running = (start, start)
        for k in range(peers):
            passed = k < place
            running = combine(running, jax.tree.map(lambda part: part[k], pieces))
            inside = jax.tree.map(lambda new, old: jnp.where(passed, new, old), running, inside)
        before = combine(inside, before)
    return before


def rms_scale(values, norm_weight):
    return (
        values
        * lax.rsqrt(jnp.mean(values * values, axis=-1, keepdims=True) + epsilon)
        * norm_weight
    )


def causal_conv(padded, weight, bias_row):
    tap_count = weight.shape[0]
    out_length = padded.shape[0] - tap_count + 1
    running = bias_row
    for k in range(tap_count):
        running = running + weight[k] * padded[k : k + out_length].astype(jnp.float32)
    return jax.nn.silu(running).astype(jnp.bfloat16)


def span_terms(x_blocks, b_blocks, c_blocks, log_decay, dt_blocks):
    cum_decay = jnp.cumsum(log_decay, axis=1)
    scores = jnp.einsum("ctgn,csgn->cgts", c_blocks, b_blocks, preferred_element_type=jnp.float32)
    length = x_blocks.shape[1]
    causal_mask = lax.broadcasted_iota(jnp.int32, (length, length), 0) >= lax.broadcasted_iota(
        jnp.int32, (length, length), 1
    )
    cum_rows = jnp.transpose(cum_decay, (0, 2, 3, 1))
    decay_gap = cum_rows[..., :, None] - cum_rows[..., None, :]
    decay_mat = jnp.where(causal_mask, jnp.exp(jnp.where(causal_mask, decay_gap, 0.0)), 0.0)
    dt_cols = jnp.transpose(dt_blocks, (0, 2, 3, 1))[..., None, :]
    mix_weight = (scores[:, :, None] * decay_mat * dt_cols).astype(jnp.bfloat16)
    intra_out = jnp.einsum(
        "cgkts,csgkp->ctgkp", mix_weight, x_blocks, preferred_element_type=jnp.float32
    )
    tail_decay = jnp.exp(cum_decay[:, -1:] - cum_decay) * dt_blocks
    scaled = (x_blocks.astype(jnp.float32) * tail_decay[..., None]).astype(jnp.bfloat16)
    fresh_state = jnp.einsum(
        "csgkp,csgn->cgkpn", scaled, b_blocks, preferred_element_type=jnp.float32
    )
    return (cum_decay, intra_out, fresh_state)


def combine(first_part, second_part):
    return (
        first_part[0] * second_part[0],
        second_part[0][..., None, None] * first_part[1] + second_part[1],
    )


def local(
    hidden_in,
    norm_gain,
    w_x,
    w_z,
    w_bc,
    w_dt,
    dt_bias,
    decay_rate,
    conv_x,
    conv_bc,
    conv_bias_x,
    conv_bias_bc,
    skip_d,
    out_gain,
    w_out,
):
    gathered = lax.all_gather(hidden_in, "tensor", axis=1, tiled=True)
    normed = rms_scale(gathered.astype(jnp.float32), norm_gain).astype(jnp.bfloat16)
    row_count = normed.shape[0]
    rim_rows = conv_x.shape[0] - 1
    groups = w_bc.shape[1]
    bc_width = w_bc.shape[2]
    state_dim = bc_width // 2
    head_count = decay_rate.shape[0]
    inner_width = w_x.shape[1]
    head_dim = inner_width // head_count
    per_group = head_count // groups
    full_x, full_z, full_bc, full_dt = side_by_side((w_x, w_z, w_bc, w_dt), SEQ, 0, 1)
    proj_x = jnp.dot(normed, full_x, preferred_element_type=jnp.float32)
    gate_z = jnp.dot(normed, full_z, preferred_element_type=jnp.float32)
    proj_bc = jnp.dot(
        normed,
        full_bc.reshape(full_bc.shape[0], groups * bc_width),
        preferred_element_type=jnp.float32,
    )
    dt_raw = jnp.dot(normed, full_dt, preferred_element_type=jnp.float32)
    proj_x = proj_x.astype(jnp.bfloat16)
    proj_bc = proj_bc.astype(jnp.bfloat16).reshape(row_count, groups, bc_width)
    edge_x, edge_bc = passed_along(
        (proj_x[row_count - rim_rows :], proj_bc[row_count - rim_rows :]), SEQ, 1
    )
    padded_x = jnp.concatenate([edge_x, proj_x], axis=0)
    padded_bc = jnp.concatenate([edge_bc, proj_bc], axis=0)
    gate_z = gate_z.astype(jnp.bfloat16)
    dt_vals = jax.nn.softplus(dt_raw + dt_bias)
    x_conv = causal_conv(padded_x, conv_x, conv_bias_x)
    bc_conv = causal_conv(padded_bc, conv_bc, conv_bias_bc)
    span_count = row_count // SPAN
    x_blocks = x_conv.reshape(span_count, SPAN, groups, per_group, head_dim)
    b_blocks = bc_conv[..., :state_dim].reshape(span_count, SPAN, groups, state_dim)
    c_blocks = bc_conv[..., state_dim:].reshape(span_count, SPAN, groups, state_dim)
    log_decay = (-dt_vals * decay_rate).reshape(span_count, SPAN, groups, per_group)
    dt_blocks = dt_vals.reshape(span_count, SPAN, groups, per_group)
    cum_decay, intra_out, fresh_state = span_terms(
        x_blocks, b_blocks, c_blocks, log_decay, dt_blocks
    )
    block_totals = cum_decay[:, -1]

    def carry_step(state_in, block_item):
        log_total, block_state = block_item
        return (jnp.exp(log_total)[..., None, None] * state_in + block_state, state_in)

    start_state = jnp.zeros((groups, per_group, head_dim, state_dim), jnp.float32)
    local_final, local_enter = lax.scan(carry_step, start_state, (block_totals, fresh_state))
    before_log = jnp.cumsum(block_totals, axis=0) - block_totals
    device_decay = jnp.exp(jnp.sum(block_totals, axis=0))
    identity = (jnp.ones_like(device_decay), jnp.zeros_like(local_final))
    c_float = c_blocks.astype(jnp.float32)
    incoming = entering((device_decay, local_final), SEQ, combine, identity)[1]
    enter_state = local_enter + jnp.exp(before_log)[..., None, None] * incoming[None]
    inter_out = jnp.exp(cum_decay)[..., None] * jnp.einsum(
        "ctgn,cgkpn->ctgkp", c_float, enter_state
    )
    skip_heads = skip_d.reshape(groups, per_group)[..., None]
    ssm_out = (intra_out + inter_out + skip_heads * x_blocks.astype(jnp.float32)).reshape(
        row_count, inner_width
    )
    gated_out = ssm_out * jax.nn.silu(gate_z.astype(jnp.float32))
    grouped = gated_out.reshape(row_count, groups, inner_width // groups)
    normed_y = (
        rms_scale(grouped, out_gain.reshape(groups, inner_width // groups))
        .reshape(row_count, inner_width)
        .astype(jnp.bfloat16)
    )
    partial_value = jnp.dot(normed_y, w_out, preferred_element_type=jnp.float32)
    summed = lax.psum_scatter(partial_value, "tensor", scatter_dimension=1, tiled=True)
    return (hidden_in.astype(jnp.float32) + summed).astype(jnp.bfloat16)


def solution(mesh):
    split = Mesh(mesh.devices.reshape(4, 8, mesh.shape["tensor"]), ("seq_0", "seq_1", "tensor"))
    in_specs = (
        P(SEQ, "tensor"),
        P(),
        P(SEQ, "tensor"),
        P(SEQ, "tensor"),
        P(SEQ, "tensor", None),
        P(SEQ, "tensor"),
        P("tensor"),
        P("tensor"),
        P(None, "tensor"),
        P(None, "tensor", None),
        P("tensor"),
        P("tensor", None),
        P("tensor"),
        P("tensor"),
        P("tensor", None),
    )
    out_specs = P(SEQ, "tensor")
    return jax.shard_map(local, mesh=split, in_specs=in_specs, out_specs=out_specs, check_vma=False)
```

profile of v0, /device:TPU:1, one launch (start us, length us, event | category | flops | bytes accessed | tf_op | source)
XLA Modules:
  0.0 395.8 jit_solution(16291231252548557750)
XLA Ops:
  6.5 0.7 all-gather.7.cloned.1.call-update
  7.3 0.8 copy.40
  8.1 2.0 pad_maximum_fusion.1
  10.2 33.4 %all-gather.7.cloned.1.call-done = bf16[384,4096]{1,0:T(8,128)(2,1)} async-done(((bf16[384,512]{1,0:T(8,128)(2,1)}), bf16[384,4096]{1,0:T(8,128)(2,1)}) %all-gather.7.cloned.1.call-update) | async-done | bytes 3145744 | tf_op jit(solution)/shard_map/all_gather | solution.py:114
  43.7 2.6 fusion.6
  46.3 154.4 %all-gather.9.cloned.1.call-done = bf16[4096,2312]{1,0:T(8,128)(2,1)} async-done(((bf16[128,2312]{1,0:T(8,128)(2,1)}), bf16[4096,2312]{1,0:T(8,128)(2,1)}) %all-gather.9.cloned.1.call-update) | async-done | bytes 18939920 | tf_op jit(solution)/shard_map/all_gather | solution.py:18
  200.7 3.2 compare_select_fusion
  204.0 0.1 copy.41
  204.1 0.2 fusion.77
  204.3 3.7 fusion.29
  208.1 1.4 collective-permute-start.1
  209.6 6.9 %fusion.23 = bf16[384,1024]{1,0:T(8,128)(2,1)S(1)} fusion(bf16[4096,2312]{1,0:T(8,128)(2,1)} %all-gather.9.cloned.1.call-done, bf16[384,4096]{1,0:T(8,128)(2,1)S(1)} %copy-done.3, f32[4096]{0:T(1024)S(1)} %copy-done.15, f32[384]{0:T(512)S(1)} %add_rsqrt_fusion.1), kind=kOutput, calls=%fused_computation.36 | convolution fusion | flops 3227910144 | bytes 12338688 | tf_op jit(solution)/shard_map/dot_general | solution.py:126
  216.5 3.2 collective-permute-start
  219.8 0.3 multiply_convert_fusion.7
  220.2 0.4 collective-permute-done
  220.5 2.2 convert_bitcast_fusion
  222.8 0.2 copy.53
  222.9 0.5 copy.44
  223.5 0.4 convolution_bitcast_fusion
  223.8 0.5 copy-done.4
  224.4 3.0 while.13
  224.4 0.8 bitcast_dynamic-update-slice_fusion.2
  225.2 0.1 bitcast_add_fusion.3
  225.4 0.9 bitcast_dynamic-update-slice_fusion.2
  226.2 0.1 bitcast_add_fusion.3
  226.4 0.8 bitcast_dynamic-update-slice_fusion.2
  227.2 0.1 bitcast_add_fusion.3
  227.3 0.8 copy-done
  228.2 0.6 dynamic-slice
  229.5 0.1 exponential_dynamic-update-slice_fusion
  229.6 14.0 %all-reduce = f32[64]{0:T(128)S(1)} all-reduce(f32[64]{0:T(128)S(1)} %exponential_dynamic-update-slice_fusion), channel_id=2, replica_groups=mesh['seq_0'=4,'seq_1'=8,'tensor'=8] {'seq_1'}, use_global_device_ids=true, to_apply=%add | all-reduce | flops 64 | bytes 512
  243.7 0.1 broadcast_select_fusion.7
  243.8 41.7 %all-gather.13.cloned.1.call-done = f32[8,8,128,128]{3,2,1,0:T(8,128)} async-done(((f32[1,8,128,128]{3,2,1,0:T(8,128)}), f32[8,8,128,128]{3,2,1,0:T(8,128)}) %all-gather.13.cloned.1.call-update) | async-done | bytes 4194320 | tf_op jit(solution)/shard_map/all_gather | solution.py:40
  285.5 3.5 fusion.54
  289.1 7.7 %all_gather.27 = f32[4,1,8]{2,1,0:T(1,128)S(1)} all-gather(f32[1,1,8]{2,1,0:T(1,128)S(1)} %get-tuple-element.105), channel_id=1, replica_groups=mesh['seq_0'=4,'seq_1'=8,'tensor'=8] {'seq_0'}, dimensions={0}, use_global_device_ids=true | all-gather | bytes 160 | tf_op jit(solution)/shard_map/all_gather | solution.py:40
  297.0 0.9 fusion.78
  297.9 0.3 copy.54
  298.2 0.5 copy.48
  298.8 3.2 fusion.35
  302.0 19.0 %all-gather.11.cloned.1.call-done = f32[4,1,8,128,128]{4,3,2,1,0:T(8,128)} async-done(((f32[1,1,8,128,128]{4,3,2,1,0:T(8,128)}), f32[4,1,8,128,128]{4,3,2,1,0:T(8,128)}) %all-gather.11.cloned.1.call-update) | async-done | bytes 2097168 | tf_op jit(solution)/shard_map/all_gather | solution.py:40
  321.0 3.7 fusion.53
  324.8 0.5 fusion.16
  325.4 0.6 copy.49
  325.9 0.1 copy-done.16
  326.1 7.4 %multiply_reduce_fusion = (f32[384]{0:T(512)S(1)}, f32[384,1024]{1,0:T(8,128)S(1)}) fusion(bf16[4096,2312]{1,0:T(8,128)(2,1)} %all-gather.9.cloned.1.call-done, bf16[384,4096]{1,0:T(8,128)(2,1)} %all-gather.7.cloned.1.call-done, f32[4096]{0:T(1024)S(1)} %copy-done.16, f32[384]{0:T(512)S(1)} %add_rsqrt_fusion.1, f32[48,8,8,128]{3,2,1,0:T(8,128)S(1)} %bitcast.191), kind=kOutput, calls=%fused_computation.29 | convolution fusion | flops 3231055360 | bytes 14699520 | tf_op jit(solution)/shard_map/dot_general | solution.py:127
  333.5 8.8 %fusion.38 = f32[384,4096]{1,0:T(8,128)} fusion(bf16[1024,4096]{1,0:T(8,128)(2,1)} %param.31, f32[384,1024]{1,0:T(8,128)S(1)} %get-tuple-element.112, f32[1024]{0:T(1024)S(1)} %copy-done.17, f32[384]{0:T(512)S(1)} %add_rsqrt_fusion), kind=kOutput, calls=%fused_computation.46 | convolution fusion | flops 3222405120 | bytes 16258560 | tf_op jit(solution)/shard_map/dot_general | solution.py:182
  342.4 44.9 %reduce-scatter.2.cloned.1.call-done = f32[384,512]{1,0:T(8,128)} async-done(((f32[384,4096]{1,0:T(8,128)}), f32[384,512]{1,0:T(8,128)}) %reduce-scatter.2.cloned.1.call-update) | async-done | bytes 786448 | tf_op jit(solution)/shard_map/reduce_scatter | solution.py:183
  387.3 2.0 add_convert_fusion
  (71 shorter events, 0.9 us)
Async XLA Ops:
  6.5 3.6 copy-start.11
  6.5 3.6 copy-start.9
  6.5 37.1 %all-gather.7.cloned.1.call-start = ((), (), s32[]{:S(2)}) async-start(), calls=%async_computation.1 | async-start | bytes 3538944 | tf_op jit(solution)/shard_map/all_gather | solution.py:114
  7.3 193.4 %all-gather.9.cloned.1.call-start = ((), (), s32[]{:S(2)}) async-start(), calls=%async_computation.2 | async-start | bytes 20545536 | tf_op jit(solution)/shard_map/all_gather | solution.py:18
  10.1 275.4 %all-gather.13.cloned.1.call-start = ((), (), s32[]{:S(2)}) async-start(), calls=%async_computation.5 | async-start | bytes 4718592 | tf_op jit(solution)/shard_map/all_gather | solution.py:40
  10.2 190.4 %copy-start.15 = (f32[4096]{0:T(1024)S(1)}, f32[4096]{0:T(1024)}, u32[]{:S(2)}) copy-start(f32[4096]{0:T(1024)} %param.18) | copy-start | bytes 49156
  10.2 190.4 %copy-start.18 = (f32[8]{0:T(128)S(1)}, f32[8]{0:T(128)}, u32[]{:S(2)}) copy-start(f32[8]{0:T(128)} %param.23) | copy-start | bytes 100
  46.3 157.6 %copy-start.14 = (f32[8]{0:T(128)S(1)}, f32[8]{0:T(128)}, u32[]{:S(2)}) copy-start(f32[8]{0:T(128)} %param.24) | copy-start | bytes 100
  204.3 5.2 %copy-start.3 = (bf16[384,4096]{1,0:T(8,128)(2,1)S(1)}, bf16[384,4096]{1,0:T(8,128)(2,1)}, u32[]{:S(2)}) copy-start(bf16[384,4096]{1,0:T(8,128)(2,1)} %all-gather.7.cloned.1.call-done) | copy-start | bytes 9437188
  208.1 11.7 %collective-permute-start.1 = (bf16[3,1,256]{2,0,1:T(4,128)(2,1)S(1)}, bf16[3,1,256]{2,0,1:T(4,128)(2,1)S(1)}, u32[]{:S(2)}, u32[]{:S(2)}) collective-permute-start(bf16[3,1,256]{2,0,1:T(4,128)(2,1)S(1)} %slice_bitcast_fusion.8), channel_id=1, source_target_pairs={{0,8},{8,16},{16,24},{24,32},{32,40},{40,48},{48,56},{56,64},{64,7... | collective-permute-start | bytes 4616 | tf_op jit(solution)/shard_map/ppermute | solution.py:26
  209.6 10.3 %copy-start.12 = (f32[1,256]{1,0:T(1,128)S(1)}, f32[1,256]{1,0:T(1,128)}, u32[]{:S(2)}) copy-start(f32[1,256]{1,0:T(1,128)} %param.28) | copy-start | bytes 3076
  209.6 10.9 %copy-start.10 = (f32[1024]{0:T(1024)S(1)}, f32[1024]{0:T(1024)}, u32[]{:S(2)}) copy-start(f32[1024]{0:T(1024)} %param.27) | copy-start | bytes 12292
  216.5 4.0 %collective-permute-start = (bf16[3,1024]{1,0:T(4,128)(2,1)S(1)}, bf16[3,1024]{1,0:T(4,128)(2,1)S(1)}, u32[]{:S(2)}, u32[]{:S(2)}) collective-permute-start(bf16[3,1024]{1,0:T(4,128)(2,1)S(1)} %slice.193), channel_id=1, source_target_pairs={{0,8},{8,16},{16,24},{24,32},{32,40},{40,48},{48,56},{56,64},{64,7... | collective-permute-start | bytes 18440 | tf_op jit(solution)/shard_map/ppermute | solution.py:26
  223.5 0.9 copy-start.4
  223.8 4.4 %copy-start.19 = (u32[256]{0:T(256)S(1)}, u32[256]{0:T(256)}, u32[]{:S(2)}) copy-start(u32[256]{0:T(256)} %constant.70) | copy-start | bytes 3076
  227.3 0.8 copy-start
  228.2 92.8 %all-gather.11.cloned.1.call-start = ((), (), s32[]{:S(2)}) async-start(), calls=%async_computation.3 | async-start | bytes 2621440 | tf_op jit(solution)/shard_map/all_gather | solution.py:40
  285.5 12.4 %copy-start.1 = (f32[48,8,8,128]{3,1,2,0:T(8,128)S(1)}, f32[48,8,8,128]{3,1,2,0:T(8,128)}, u32[]{:S(2)}) copy-start(f32[48,8,8,128]{3,1,2,0:T(8,128)} %get-tuple-element.80) | copy-start | bytes 4718596
  289.1 98.2 %reduce-scatter.2.cloned.1.call-start = ((), (), s32[]{:S(2)}) async-start(), calls=%async_computation.4 | async-start | bytes 7077888 | tf_op jit(solution)/shard_map/reduce_scatter | solution.py:183
  298.7 22.2 %copy-start.2 = (f32[1,1,8,128,128]{4,3,2,1,0:T(8,128)S(1)}, f32[1,1,8,128,128]{4,3,2,1,0:T(8,128)}, u32[]{:S(2)}) copy-start(f32[1,1,8,128,128]{4,3,2,1,0:T(8,128)} %get-tuple-element.78) | copy-start | bytes 1572868
  298.8 22.2 %copy-start.5 = (f32[1,1,8,128,128]{4,3,2,1,0:T(8,128)S(1)}, f32[1,1,8,128,128]{4,3,2,1,0:T(8,128)}, u32[]{:S(2)}) copy-start(f32[1,1,8,128,128]{4,3,2,1,0:T(8,128)} %get-tuple-element.79) | copy-start | bytes 1572868
  321.0 3.8 copy-start.7
  321.0 3.8 copy-start.8
  321.0 3.8 copy-start.13
  325.3 0.7 copy-start.16
  326.1 7.5 %copy-start.17 = (f32[1024]{0:T(1024)S(1)}, f32[1024]{0:T(1024)}, u32[]{:S(2)}) copy-start(f32[1024]{0:T(1024)} %param.30) | copy-start | bytes 12292
  342.4 44.9 %copy-start.6 = (bf16[384,512]{1,0:T(8,128)(2,1)S(1)}, bf16[384,512]{1,0:T(8,128)(2,1)}, u32[]{:S(2)}) copy-start(bf16[384,512]{1,0:T(8,128)(2,1)} %param.17) | copy-start | bytes 1179652
Sparse Core Ops, SparseCore 0:
  9.2 34.4 all-gather.6
  46.2 154.3 all-gather.8
  228.3 57.1 all-gather.12
  289.2 31.7 all-gather.10
  342.5 44.7 reduce-scatter.1
where the time goes:
time: 396 us
  waiting for transfers between devices  295 us (74%)
  matrix products  35.2 us (9%)
  blocking collectives  21.8 us (6%)
  other arithmetic  19.8 us (5%)
  between operations  14.2 us (4%)
  local copies, waits for them, and re-layouts  5.45 us (1%)
  starting transfers between devices  4.78 us (1%)
    all_gather x1, waiting for transfers between devices, side_by_side(): whole = lax.all_gather(both, axis, axis=dim, tiled=True)  154 us
    all_gather x2, waiting for transfers between devices, entering(): pieces = jax.tree.map(lambda part: lax.all_gather(part, axis), running)  60.7 us
    reduce_scatter x1, waiting for transfers between devices, local(): lax.psum_scatter(partial_value, 'tensor', scatter_dimension=1, tiled=True)  44.9 us
    all_gather x1, waiting for transfers between devices, local(): gathered = lax.all_gather(hidden_in, 'tensor', axis=1, tiled=True)  33.4 us
    unnamed x1, blocking collectives  14 us
    dot_general x1, matrix products, local(): partial_value = jnp.dot(normed_y, w_out, preferred_element_type=jnp.float32)  8.85 us
  transfers between devices with their start and end apart: 7, of which 6 were waited for; matrix products, arithmetic and copies ran while one was open for 5% of the time, Pallas kernels for 0%

commit v1 on v0

--- a/solution.py
+++ b/solution.py
@@ -8,6 +8,23 @@
 SPAN = 128
 SEQ = ("seq_0", "seq_1")
 epsilon = 1e-05
+
+
+def laid_out(parts, dim):
+    shape = list(parts.shape[1:])
+    shape[dim] *= parts.shape[0]
+    return jnp.moveaxis(parts, 0, dim).reshape(shape)
+
+
+def doubled(x, axis):
+    size, index = (lax.axis_size(axis), lax.axis_index(axis))
+    tiles, bit = (x[None], 1)
+    while bit < size:
+        other = lax.ppermute(tiles, axis, [(i, i ^ bit) for i in range(size)])
+        low = index & bit == 0
+        tiles = jnp.concatenate([jnp.where(low, tiles, other), jnp.where(low, other, tiles)])
+        bit *= 2
+    return tiles
 
 
 def side_by_side(arrays, axis, dim, along):
@@ -111,7 +128,7 @@
     out_gain,
     w_out,
 ):
-    gathered = lax.all_gather(hidden_in, "tensor", axis=1, tiled=True)
+    gathered = laid_out(doubled(hidden_in, "tensor"), 1)
     normed = rms_scale(gathered.astype(jnp.float32), norm_gain).astype(jnp.bfloat16)
     row_count = normed.shape[0]
     rim_rows = conv_x.shape[0] - 1

time: 396 us -> 368 us (0.929)
  waiting for transfers between devices: 295 us -> 249 us
  other arithmetic: 19.8 us -> 28.3 us
  starting transfers between devices: 4.78 us -> 9.3 us
  local copies, waits for them, and re-layouts: 5.45 us -> 9.42 us
    all_gather x1, waiting for transfers between devices: 154 us -> 90.1 us  [side_by_side(): whole = lax.all_gather(both, axis, axis=dim, tiled=True)]
    ppermute x0 -> x3, waiting for transfers between devices: none -> 55.5 us  [doubled(): other = lax.ppermute(tiles, axis, [(i, i ^ bit) for i in range(size)])]
    all_gather x1 -> x0, waiting for transfers between devices: 33.4 us -> none  [local(): gathered = lax.all_gather(hidden_in, 'tensor', axis=1, tiled=True)]
    ppermute x0 -> x3, starting transfers between devices: none -> 4.57 us  [doubled(): other = lax.ppermute(tiles, axis, [(i, i ^ bit) for i in range(size)])]
  transfers between devices with their start and end apart: 7 -> 9, of which waited for: 6 -> 7; matrix products, arithmetic and copies ran while one was open for 5% -> 7% of each run, Pallas kernels for 0% -> 0%
where the time goes in v1:
time: 368 us
  waiting for transfers between devices  249 us (68%)
  matrix products  36.5 us (10%)
  other arithmetic  28.3 us (8%)
  blocking collectives  20.9 us (6%)
  between operations  14.5 us (4%)
  local copies, waits for them, and re-layouts  9.42 us (3%)
  starting transfers between devices  9.3 us (3%)
    all_gather x1, waiting for transfers between devices, side_by_side(): whole = lax.all_gather(both, axis, axis=dim, tiled=True)  90.1 us
    all_gather x2, waiting for transfers between devices, entering(): pieces = jax.tree.map(lambda part: lax.all_gather(part, axis), running)  58.1 us
    ppermute x3, waiting for transfers between devices, doubled(): other = lax.ppermute(tiles, axis, [(i, i ^ bit) for i in range(size)])  55.5 us
    reduce_scatter x1, waiting for transfers between devices, local(): lax.psum_scatter(partial_value, 'tensor', scatter_dimension=1, tiled=True)  44.9 us
    unnamed x1, blocking collectives  13.2 us
    dot_general x1, matrix products, local(): partial_value = jnp.dot(normed_y, w_out, preferred_element_type=jnp.float32)  8.82 us
    dot_general x1, matrix products, local(): gate_z = jnp.dot(normed, full_z, preferred_element_type=jnp.float32)  7.89 us
    all_gather x1, blocking collectives, entering(): pieces = jax.tree.map(lambda part: lax.all_gather(part, axis), running)  7.72 us
  transfers between devices with their start and end apart: 9, of which 7 were waited for; matrix products, arithmetic and copies ran while one was open for 7% of the time, Pallas kernels for 0%

profile of v1, /device:TPU:1, one launch (start us, length us, event | category | flops | bytes accessed | tf_op | source)
XLA Modules:
  0.0 367.6 jit_solution(7176093356508618887)
XLA Ops:
  6.5 0.8 copy.55
  7.4 1.9 pad_maximum_fusion.3
  9.6 3.3 collective-permute-start
  12.9 1.3 collective-permute-done
  14.6 18.8 %collective-permute-done.1 = bf16[2,384,512]{1,2,0:T(8,128)(2,1)} collective-permute-done((bf16[2,384,512]{1,2,0:T(8,128)(2,1)S(1)}, bf16[2,384,512]{1,2,0:T(8,128)(2,1)}, u32[]{:S(2)}, u32[]{:S(2)}) %collective-permute-start.1) | collective-permute-done | bytes 786464 | tf_op jit(solution)/shard_map/ppermute | solution.py:23
  33.4 1.3 broadcast_select_fusion.3
  34.7 1.3 pad_maximum_fusion
  36.1 1.2 collective-permute-start.2
  37.3 35.3 %collective-permute-done.2 = bf16[4,384,512]{1,2,0:T(8,128)(2,1)} collective-permute-done((bf16[4,384,512]{1,2,0:T(8,128)(2,1)}, bf16[4,384,512]{1,2,0:T(8,128)(2,1)}, u32[]{:S(2)}, u32[]{:S(2)}) %collective-permute-start.2) | collective-permute-done | bytes 1572896 | tf_op jit(solution)/shard_map/ppermute | solution.py:23
  72.6 1.8 broadcast_select_fusion.1
  74.4 0.8 multiply_reduce_fusion
  76.0 2.6 fusion.7
  78.5 90.1 %all-gather.6.cloned.1.call-done = bf16[4096,2312]{1,0:T(8,128)(2,1)} async-done(((bf16[128,2312]{1,0:T(8,128)(2,1)}), bf16[4096,2312]{1,0:T(8,128)(2,1)}) %all-gather.6.cloned.1.call-update) | async-done | bytes 18939920 | tf_op jit(solution)/shard_map/all_gather | solution.py:35
  168.6 2.7 compare_select_fusion
  171.7 0.6 slice_reduce_fusion
  172.4 3.7 %fusion.28 = bf16[384,256]{1,0:T(8,128)(2,1)S(1)} fusion(bf16[384,4096]{0,1:T(8,128)(2,1)} %fusion.7, bf16[4096,2312]{1,0:T(8,128)(2,1)} %all-gather.6.cloned.1.call-done), kind=kOutput, calls=%fused_computation.41 | convolution fusion | flops 805404672 | bytes 5439488 | tf_op jit(solution)/shard_map/dot_general | solution.py:145
  176.1 1.4 collective-permute-start.4
  177.6 6.0 %fusion.22 = bf16[384,1024]{1,0:T(8,128)(2,1)S(1)} fusion(bf16[384,4096]{0,1:T(8,128)(2,1)S(1)} %copy-done.1, bf16[4096,2312]{1,0:T(8,128)(2,1)} %all-gather.6.cloned.1.call-done), kind=kOutput, calls=%fused_computation.39 | convolution fusion | flops 3221618688 | bytes 12320768 | tf_op jit(solution)/shard_map/dot_general | solution.py:143
  183.6 3.2 collective-permute-start.3
  186.8 0.6 bitcast_exponential_fusion
  187.7 0.7 fusion.69
  188.4 2.2 convert_bitcast_fusion
  190.8 0.5 copy.59
  191.4 1.3 convolution_bitcast_fusion
  192.7 3.0 while.13
  192.8 0.8 bitcast_dynamic-update-slice_fusion.2
  193.7 0.8 bitcast_dynamic-update-slice_fusion.2
  194.7 0.8 bitcast_dynamic-update-slice_fusion.2
  195.7 0.8 copy-done
  196.6 0.7 dynamic-slice
  198.1 13.2 %all-reduce = f32[64]{0:T(128)S(1)} all-reduce(f32[64]{0:T(128)S(1)} %exponential_dynamic-update-slice_fusion), channel_id=2, replica_groups=mesh['seq_0'=4,'seq_1'=8,'tensor'=8] {'seq_1'}, use_global_device_ids=true, to_apply=%add | all-reduce | flops 64 | bytes 512
  211.4 0.6 broadcast_select_fusion.13
  212.0 41.1 %all-gather.10.cloned.1.call-done = f32[8,8,128,128]{3,2,1,0:T(8,128)} async-done(((f32[1,8,128,128]{3,2,1,0:T(8,128)}), f32[8,8,128,128]{3,2,1,0:T(8,128)}) %all-gather.10.cloned.1.call-update) | async-done | bytes 4194320 | tf_op jit(solution)/shard_map/all_gather | solution.py:57
  253.1 3.5 fusion.53
  256.7 0.6 iota_compare_fusion
  257.3 7.7 %all_gather.23 = f32[4,1,8]{2,1,0:T(1,128)S(1)} all-gather(f32[1,1,8]{2,1,0:T(1,128)S(1)} %get-tuple-element.116), channel_id=1, replica_groups=mesh['seq_0'=4,'seq_1'=8,'tensor'=8] {'seq_0'}, dimensions={0}, use_global_device_ids=true | all-gather | bytes 160 | tf_op jit(solution)/shard_map/all_gather | solution.py:57
  265.1 0.7 copy.57
  265.8 0.6 slice_bitcast_fusion.11
  266.4 0.9 fusion.73
  268.3 3.3 fusion.34
  271.6 17.0 %all-gather.8.cloned.1.call-done = f32[4,1,8,128,128]{4,3,2,1,0:T(8,128)} async-done(((f32[1,1,8,128,128]{4,3,2,1,0:T(8,128)}), f32[4,1,8,128,128]{4,3,2,1,0:T(8,128)}) %all-gather.8.cloned.1.call-update) | async-done | bytes 2097168 | tf_op jit(solution)/shard_map/all_gather | solution.py:57
  288.7 3.7 %fusion.52 = f32[8,128,128]{2,1,0:T(8,128)S(1)} fusion(f32[4,1,8,128,128]{4,3,2,1,0:T(8,128)} %all-gather.8.cloned.1.call-done, f32[1,1,8,128,128]{4,3,2,1,0:T(8,128)S(1)} %copy-done.4, f32[1,1,8,128,128]{4,3,2,1,0:T(8,128)S(1)} %copy-done.6, f32[8,8,128,128]{3,2,1,0:T(8,128)} %all-gather.10.cloned.1.call-done, f32[8]{0:T(128)S(1)} %copy-done.24, ...), kind=kLoop, calls=%fused_computation.71 | loop fusion | flops 4194304 | bytes 6816108 | tf_op jit(solution)/shard_map/mul | solution.py:184
  292.5 1.7 fusion.15
  294.2 3.2 copy.64
  297.4 7.9 %multiply_reduce_fusion.1 = (f32[384]{0:T(512)S(1)}, f32[384,1024]{1,0:T(8,128)S(1)}) fusion(bf16[384,4096]{0,1:T(8,128)(2,1)S(1)} %copy-done.2, bf16[4096,2312]{1,0:T(8,128)(2,1)} %all-gather.6.cloned.1.call-done, f32[48,8,8,128]{3,2,1,0:T(8,128)} %bitcast.206), kind=kOutput, calls=%fused_computation.30 | convolution fusion | flops 3224763904 | bytes 14681600 | tf_op jit(solution)/shard_map/dot_general | solution.py:144
  305.3 8.8 %fusion.37 = f32[384,4096]{1,0:T(8,128)} fusion(bf16[1024,4096]{1,0:T(8,128)(2,1)} %param.31, f32[384,1024]{1,0:T(8,128)S(1)} %get-tuple-element.123, f32[1024]{0:T(1024)S(1)} %copy-done.40, f32[384]{0:T(512)S(1)} %add_rsqrt_fusion), kind=kOutput, calls=%fused_computation.49 | convolution fusion | flops 3222405120 | bytes 16258560 | tf_op jit(solution)/shard_map/dot_general | solution.py:199
  314.2 44.9 %reduce-scatter.2.cloned.1.call-done = f32[384,512]{1,0:T(8,128)} async-done(((f32[384,4096]{1,0:T(8,128)}), f32[384,512]{1,0:T(8,128)}) %reduce-scatter.2.cloned.1.call-update) | async-done | bytes 786448 | tf_op jit(solution)/shard_map/reduce_scatter | solution.py:200
  359.1 2.0 add_convert_fusion
  (126 shorter events, 3.9 us)
Async XLA Ops:
  6.5 2.9 copy-start.7
  6.5 162.0 %all-gather.6.cloned.1.call-start = ((), (), s32[]{:S(2)}) async-start(), calls=%async_computation.1 | async-start | bytes 20545536 | tf_op jit(solution)/shard_map/all_gather | solution.py:35
  9.4 243.7 %all-gather.10.cloned.1.call-start = ((), (), s32[]{:S(2)}) async-start(), calls=%async_computation.4 | async-start | bytes 4718592 | tf_op jit(solution)/shard_map/all_gather | solution.py:57
  9.6 4.6 %collective-permute-start = (bf16[1,384,512]{1,2,0:T(8,128)(2,1)S(1)}, bf16[1,384,512]{1,2,0:T(8,128)(2,1)S(1)}, u32[]{:S(2)}, u32[]{:S(2)}) collective-permute-start(bf16[1,384,512]{1,2,0:T(8,128)(2,1)S(1)} %bitcast.207), channel_id=1, source_target_pairs={{0,1},{1,0},{2,3},{3,2},{4,5},{5,4},{6,7},{7,6},{8,9},{9,8},{10,11... | collective-permute-start | bytes 1179656 | tf_op jit(solution)/shard_map/ppermute | solution.py:23
  14.4 18.9 %collective-permute-start.1 = (bf16[2,384,512]{1,2,0:T(8,128)(2,1)S(1)}, bf16[2,384,512]{1,2,0:T(8,128)(2,1)}, u32[]{:S(2)}, u32[]{:S(2)}) collective-permute-start(bf16[2,384,512]{1,2,0:T(8,128)(2,1)S(1)} %pad_maximum_fusion.2), channel_id=1, source_target_pairs={{0,2},{1,3},{2,0},{3,1},{4,6},{5,7},{6,4},{7,5},{8,10},{9,11},{10,... | collective-permute-start | bytes 2359304 | tf_op jit(solution)/shard_map/ppermute | solution.py:23
  34.7 2.6 copy-start.30
  34.7 2.5 copy-start.14
  36.1 36.6 %collective-permute-start.2 = (bf16[4,384,512]{1,2,0:T(8,128)(2,1)}, bf16[4,384,512]{1,2,0:T(8,128)(2,1)}, u32[]{:S(2)}, u32[]{:S(2)}) collective-permute-start(bf16[4,384,512]{1,2,0:T(8,128)(2,1)} %pad_maximum_fusion), channel_id=1, source_target_pairs={{0,4},{1,5},{2,6},{3,7},{4,0},{5,1},{6,2},{7,3},{8,12},{9,13},{10,... | collective-permute-start | bytes 4718600 | tf_op jit(solution)/shard_map/ppermute | solution.py:23
  76.0 92.6 %copy-start.16 = (f32[8]{0:T(128)S(1)}, f32[8]{0:T(128)}, u32[]{:S(2)}) copy-start(f32[8]{0:T(128)} %param.23) | copy-start | bytes 100
  78.5 92.8 %copy-start.38 = (f32[8]{0:T(128)S(1)}, f32[8]{0:T(128)}, u32[]{:S(2)}) copy-start(f32[8]{0:T(128)} %param.24) | copy-start | bytes 100
  172.4 5.2 %copy-start.1 = (bf16[384,4096]{0,1:T(8,128)(2,1)S(1)}, bf16[384,4096]{0,1:T(8,128)(2,1)}, u32[]{:S(2)}) copy-start(bf16[384,4096]{0,1:T(8,128)(2,1)} %fusion.7) | copy-start | bytes 9437188
  176.1 11.3 %copy-start.36 = (f32[1,256]{1,0:T(1,128)S(1)}, f32[1,256]{1,0:T(1,128)}, u32[]{:S(2)}) copy-start(f32[1,256]{1,0:T(1,128)} %param.28) | copy-start | bytes 3076
  176.1 12.3 %copy-start.29 = (f32[1024]{0:T(1024)S(1)}, f32[1024]{0:T(1024)}, u32[]{:S(2)}) copy-start(f32[1024]{0:T(1024)} %param.27) | copy-start | bytes 12292
  176.1 11.3 %collective-permute-start.4 = (bf16[3,1,256]{2,0,1:T(4,128)(2,1)S(1)}, bf16[3,1,256]{2,0,1:T(4,128)(2,1)S(1)}, u32[]{:S(2)}, u32[]{:S(2)}) collective-permute-start(bf16[3,1,256]{2,0,1:T(4,128)(2,1)S(1)} %slice_bitcast_fusion.8), channel_id=1, source_target_pairs={{0,8},{8,16},{16,24},{24,32},{32,40},{40,48},{48,56},{56,64},{64,7... | collective-permute-start | bytes 4616 | tf_op jit(solution)/shard_map/ppermute | solution.py:43
  183.6 4.8 %collective-permute-start.3 = (bf16[3,1024]{1,0:T(4,128)(2,1)S(1)}, bf16[3,1024]{1,0:T(4,128)(2,1)S(1)}, u32[]{:S(2)}, u32[]{:S(2)}) collective-permute-start(bf16[3,1024]{1,0:T(4,128)(2,1)S(1)} %slice.193), channel_id=1, source_target_pairs={{0,8},{8,16},{16,24},{24,32},{32,40},{40,48},{48,56},{56,64},{64,7... | collective-permute-start | bytes 18440 | tf_op jit(solution)/shard_map/ppermute | solution.py:43
  192.7 3.9 %copy-start.41 = (u32[256]{0:T(256)S(1)}, u32[256]{0:T(256)}, u32[]{:S(2)}) copy-start(u32[256]{0:T(256)} %constant.72) | copy-start | bytes 3076
  192.7 5.3 %copy-start.39 = (f32[8]{0:T(128)S(1)}, f32[8]{0:T(128)}, u32[]{:S(2)}) copy-start(f32[8]{0:T(128)} %get-tuple-element.93) | copy-start | bytes 100
  196.5 92.1 %all-gather.8.cloned.1.call-start = ((), (), s32[]{:S(2)}) async-start(), calls=%async_computation.2 | async-start | bytes 2621440 | tf_op jit(solution)/shard_map/all_gather | solution.py:57
  211.4 45.2 %copy-start.17 = (f32[8]{0:T(128)}, f32[8]{0:T(128)S(1)}, u32[]{:S(2)}) copy-start(f32[8]{0:T(128)S(1)} %get-tuple-element.118) | copy-start | bytes 100
  211.4 45.2 %copy-start.19 = (f32[8]{0:T(128)}, f32[8]{0:T(128)S(1)}, u32[]{:S(2)}) copy-start(f32[8]{0:T(128)S(1)} %get-tuple-element.119) | copy-start | bytes 100
  211.4 45.2 %copy-start.21 = (f32[8]{0:T(128)}, f32[8]{0:T(128)S(1)}, u32[]{:S(2)}) copy-start(f32[8]{0:T(128)S(1)} %get-tuple-element.121) | copy-start | bytes 100
  212.0 44.6 %copy-start.23 = (f32[8]{0:T(128)}, f32[8]{0:T(128)S(1)}, u32[]{:S(2)}) copy-start(f32[8]{0:T(128)S(1)} %get-tuple-element.113) | copy-start | bytes 100
  212.0 44.6 %copy-start.25 = (f32[8]{0:T(128)}, f32[8]{0:T(128)S(1)}, u32[]{:S(2)}) copy-start(f32[8]{0:T(128)S(1)} %get-tuple-element.114) | copy-start | bytes 100
  212.0 44.7 %copy-start.27 = (f32[8]{0:T(128)}, f32[8]{0:T(128)S(1)}, u32[]{:S(2)}) copy-start(f32[8]{0:T(128)S(1)} %get-tuple-element.115) | copy-start | bytes 100
  253.1 13.3 %copy-start.10 = (bf16[384,1,128]{2,0,1:T(8,128)(2,1)S(1)}, bf16[384,1,128]{2,0,1:T(8,128)(2,1)}, u32[]{:S(2)}) copy-start(bf16[384,1,128]{2,0,1:T(8,128)(2,1)} %get-tuple-element.96) | copy-start | bytes 294916
  253.1 13.3 %copy-start.11 = (bf16[384,1,128]{2,0,1:T(8,128)(2,1)S(1)}, bf16[384,1,128]{2,0,1:T(8,128)(2,1)}, u32[]{:S(2)}) copy-start(bf16[384,1,128]{2,0,1:T(8,128)(2,1)} %get-tuple-element.97) | copy-start | bytes 294916
  253.1 14.2 %copy-start.3 = (f32[48,8,8,128]{3,1,2,0:T(8,128)S(1)}, f32[48,8,8,128]{3,1,2,0:T(8,128)}, u32[]{:S(2)}) copy-start(f32[48,8,8,128]{3,1,2,0:T(8,128)} %get-tuple-element.85) | copy-start | bytes 4718596
  256.7 102.4 %reduce-scatter.2.cloned.1.call-start = ((), (), s32[]{:S(2)}) async-start(), calls=%async_computation.3 | async-start | bytes 7077888 | tf_op jit(solution)/shard_map/reduce_scatter | solution.py:200
  268.1 20.5 %copy-start.4 = (f32[1,1,8,128,128]{4,3,2,1,0:T(8,128)S(1)}, f32[1,1,8,128,128]{4,3,2,1,0:T(8,128)}, u32[]{:S(2)}) copy-start(f32[1,1,8,128,128]{4,3,2,1,0:T(8,128)} %get-tuple-element.83) | copy-start | bytes 1572868
  268.1 20.5 %copy-start.6 = (f32[1,1,8,128,128]{4,3,2,1,0:T(8,128)S(1)}, f32[1,1,8,128,128]{4,3,2,1,0:T(8,128)}, u32[]{:S(2)}) copy-start(f32[1,1,8,128,128]{4,3,2,1,0:T(8,128)} %get-tuple-element.84) | copy-start | bytes 1572868
  268.1 20.5 %copy-start.18 = (f32[8]{0:T(128)S(1)}, f32[8]{0:T(128)}, u32[]{:S(2)}) copy-start(f32[8]{0:T(128)} %copy-done.17) | copy-start | bytes 100
  268.2 20.4 %copy-start.20 = (f32[8]{0:T(128)S(1)}, f32[8]{0:T(128)}, u32[]{:S(2)}) copy-start(f32[8]{0:T(128)} %copy-done.19) | copy-start | bytes 100
  268.2 20.4 %copy-start.22 = (f32[8]{0:T(128)S(1)}, f32[8]{0:T(128)}, u32[]{:S(2)}) copy-start(f32[8]{0:T(128)} %copy-done.21) | copy-start | bytes 100
  268.2 20.4 %copy-start.24 = (f32[8]{0:T(128)S(1)}, f32[8]{0:T(128)}, u32[]{:S(2)}) copy-start(f32[8]{0:T(128)} %copy-done.23) | copy-start | bytes 100
  268.2 20.4 %copy-start.26 = (f32[8]{0:T(128)S(1)}, f32[8]{0:T(128)}, u32[]{:S(2)}) copy-start(f32[8]{0:T(128)} %copy-done.25) | copy-start | bytes 100
  268.2 20.4 %copy-start.28 = (f32[8]{0:T(128)S(1)}, f32[8]{0:T(128)}, u32[]{:S(2)}) copy-start(f32[8]{0:T(128)} %copy-done.27) | copy-start | bytes 100
  268.2 20.4 %copy-start.31 = (f32[8]{0:T(128)S(1)}, f32[8]{0:T(128)}, u32[]{:S(2)}) copy-start(f32[8]{0:T(128)} %get-tuple-element.112) | copy-start | bytes 100
  268.2 20.4 %copy-start.32 = (f32[8]{0:T(128)S(1)}, f32[8]{0:T(128)}, u32[]{:S(2)}) copy-start(f32[8]{0:T(128)} %get-tuple-element.108) | copy-start | bytes 100
  268.2 20.4 %copy-start.33 = (f32[8]{0:T(128)S(1)}, f32[8]{0:T(128)}, u32[]{:S(2)}) copy-start(f32[8]{0:T(128)} %get-tuple-element.109) | copy-start | bytes 100
  268.2 20.4 %copy-start.34 = (f32[8]{0:T(128)S(1)}, f32[8]{0:T(128)}, u32[]{:S(2)}) copy-start(f32[8]{0:T(128)} %get-tuple-element.110) | copy-start | bytes 100
  268.2 20.4 %copy-start.35 = (f32[8]{0:T(128)S(1)}, f32[8]{0:T(128)}, u32[]{:S(2)}) copy-start(f32[8]{0:T(128)} %get-tuple-element.111) | copy-start | bytes 100
  288.7 3.8 %copy-start.8 = (f32[3,1,8,128,128]{4,3,2,1,0:T(8,128)S(1)}, f32[3,1,8,128,128]{4,3,2,1,0:T(8,128)}, u32[]{:S(2)}) copy-start(f32[3,1,8,128,128]{4,3,2,1,0:T(8,128)} %get-tuple-element.33) | copy-start | bytes 4718596
  288.7 3.8 %copy-start.9 = (f32[3,8,128,128]{3,2,1,0:T(8,128)S(1)}, f32[3,8,128,128]{3,2,1,0:T(8,128)}, u32[]{:S(2)}) copy-start(f32[3,8,128,128]{3,2,1,0:T(8,128)} %fusion.34) | copy-start | bytes 4718596
  288.7 3.8 %copy-start.12 = (bf16[384,1,128]{2,0,1:T(8,128)(2,1)S(1)}, bf16[384,1,128]{2,0,1:T(8,128)(2,1)}, u32[]{:S(2)}) copy-start(bf16[384,1,128]{2,0,1:T(8,128)(2,1)} %get-tuple-element.97) | copy-start | bytes 294916
  288.7 3.8 %copy-start.13 = (f32[3,128,8]{1,2,0:T(8,128)S(1)}, f32[3,128,8]{1,2,0:T(8,128)}, u32[]{:S(2)}) copy-start(f32[3,128,8]{1,2,0:T(8,128)} %get-tuple-element.102) | copy-start | bytes 36868
  288.7 3.8 %copy-start.37 = (f32[8]{0:T(128)S(1)}, f32[8]{0:T(128)}, u32[]{:S(2)}) copy-start(f32[8]{0:T(128)} %param.29) | copy-start | bytes 100
  294.2 3.2 copy-start.2
  297.4 7.9 %copy-start.40 = (f32[1024]{0:T(1024)S(1)}, f32[1024]{0:T(1024)}, u32[]{:S(2)}) copy-start(f32[1024]{0:T(1024)} %param.30) | copy-start | bytes 12292
  (3 other events, 2.9 us)
Sparse Core Ops, SparseCore 0:
  9.9 158.6 all-gather.5
  196.6 56.3 all-gather.9
  256.8 31.7 all-gather.7
  314.3 44.7 reduce-scatter.1
